TPU v7x, 512 devices: a whole 4x8x8 slice. The times are simulated.
512 devices in a mesh: orb: 4 (over x), gx: 8 (over y), gyz: 16 (over z, core).
Axes of the slice: x: 4, y: 8, z: 8, core: 2. Of those that a mesh axis runs over, the one named last changes fastest.
Arguments:
- orbitals: float32 [2, 12, 128, 128, 128], P(None, 'orb', 'gx', 'gyz'), parts along dimension 1, may hold values from -12 to 12
- potential: float32 [128, 128, 128], P('gx', 'gyz'), may hold values from -8 to 60
Outputs:
- evolved: float32 [2, 12, 128, 128, 128], P(None, 'orb', 'gx', 'gyz'), parts along dimension 1
- residual: float32 [2, 12, 128, 128, 128], P(None, 'orb', 'gx', 'gyz'), parts along dimension 1
There are 4 independent parts, one for each index of `orb`. A program takes and returns all parts, laid end to end along the dimension named above; an argument that names none is the same for every part. Nothing has to cross between parts.
All inputs are finite; a program needn't handle non-finite values.
Results may differ from a plain program's by a relative error of at most 0.0003.
Values sent between devices are 32-bit elements; how exact they have to be, the bound alone decides.
A program may use at most 64 MiB of HBM per device.

v0:
```python
import jax
import jax.numpy as jnp
from jax import lax
from jax.sharding import Mesh
from jax.sharding import PartitionSpec as P

ITERS = 4
GX_GYZ = ("gx", "gyz_0", "gyz_1")
GYZ = ("gyz_0", "gyz_1")
SPACING = 0.25
HALF_STEP = 0.05
COEFF_NEAR = 4.0 / 3.0
COEFF_FAR = -1.0 / 12.0
COEFF_SELF = -2.5


def padded_2(array, sides, width):
    edges = {}
    for axis, dim in sides:
        size, length = (lax.axis_size(axis), array.shape[dim])
        up = [(i, (i + 1) % size) for i in range(size - 1)]
        last = lax.slice_in_dim(array, length - width, length, axis=dim)
        leading = lax.slice_in_dim(array, 0, width, axis=dim)
        edges[dim] = (
            lax.ppermute(last, axis, up),
            lax.ppermute(leading, axis, [(b, a) for a, b in up]),
        )
    done = []
    for _, dim in sides:
        low, high = edges[dim]
        around = [(width, width) if d in done else (0, 0) for d in range(array.ndim)]
        array = jnp.concatenate([jnp.pad(low, around), array, jnp.pad(high, around)], axis=dim)
        done.append(dim)
    return array


def by_axis(array, axes):
    for axis in axes:
        array = lax.psum(array, axis)
    return array


def laplace_apply(padded, potential):
    extent = (padded.shape[2] - 4, padded.shape[3] - 4, padded.shape[4] - 4)

    def window(shift_x, shift_y, shift_z):
        return padded[
            :,
            :,
            2 + shift_x : 2 + shift_x + extent[0],
            2 + shift_y : 2 + shift_y + extent[1],
            2 + shift_z : 2 + shift_z + extent[2],
        ]

    center = window(0, 0, 0)
    summed = 3.0 * COEFF_SELF * center
    for offset, weight in ((1, COEFF_NEAR), (2, COEFF_FAR)):
        summed = summed + weight * (
            window(offset, 0, 0)
            + window(-offset, 0, 0)
            + window(0, offset, 0)
            + window(0, -offset, 0)
            + window(0, 0, offset)
            + window(0, 0, -offset)
        )
    return -0.5 / SPACING**2 * summed + potential * center


def pad_depth(vector):
    return jnp.pad(vector, ((0, 0), (0, 0), (0, 0), (0, 0), (2, 2)))


def system(vector, applied):
    return jnp.stack([vector[0] - HALF_STEP * applied[1], vector[1] + HALF_STEP * applied[0]])


def precondition(vector, potential):
    diagonal = HALF_STEP * (3.75 / SPACING**2 + potential)
    divisor = 1.0 + diagonal * diagonal
    return jnp.stack(
        [(vector[0] + diagonal * vector[1]) / divisor, (vector[1] - diagonal * vector[0]) / divisor]
    )


def braket(left, right):
    real_part = jnp.sum(left[0] * right[0] + left[1] * right[1], axis=(1, 2, 3))
    imag_part = jnp.sum(left[0] * right[1] - left[1] * right[0], axis=(1, 2, 3))
    return (real_part, imag_part)


def times_complex(first, second):
    return (
        first[0] * second[0] - first[1] * second[1],
        first[0] * second[1] + first[1] * second[0],
    )


def divide_complex(first, second):
    modulus = second[0] * second[0] + second[1] * second[1]
    return (
        (first[0] * second[0] + first[1] * second[1]) / modulus,
        (first[1] * second[0] - first[0] * second[1]) / modulus,
    )


def scale_complex(coeff, vector):
    real_coef = coeff[0][:, None, None, None]
    imag_coef = coeff[1][:, None, None, None]
    return jnp.stack(
        [
            real_coef * vector[0] - imag_coef * vector[1],
            real_coef * vector[1] + imag_coef * vector[0],
        ]
    )


def shards(orbitals, potential):

    def apply_shallow(vector):
        padded = padded_2(vector, (("gx", 2), (GYZ, 3)), 2)
        return laplace_apply(pad_depth(padded), potential)

    h_orbitals = apply_shallow(orbitals)
    residual = jnp.stack([2.0 * HALF_STEP * h_orbitals[1], -2.0 * HALF_STEP * h_orbitals[0]])
    evolved = orbitals
    shadow = residual
    direction = residual
    rho_now = jax.tree.map(lambda part: by_axis(part, GX_GYZ), braket(shadow, residual))
    for iteration in range(ITERS):
        dir_hat = precondition(direction, potential)
        image = system(dir_hat, apply_shallow(dir_hat))
        alpha_step = divide_complex(
            rho_now, jax.tree.map(lambda part: by_axis(part, GX_GYZ), braket(shadow, image))
        )
        half_step = residual - scale_complex(alpha_step, image)
        half_hat = precondition(half_step, potential)
        second = system(half_hat, apply_shallow(half_hat))
        cross_local = braket(second, half_step)
        norm_local = jnp.sum(second * second, axis=(0, 2, 3, 4))
        shadow_half = braket(shadow, half_step)
        shadow_second = braket(shadow, second)
        summed = (
            by_axis(cross_local[0], GX_GYZ),
            by_axis(cross_local[1], GX_GYZ),
            by_axis(norm_local, GX_GYZ),
            by_axis(shadow_half[0], GX_GYZ),
            by_axis(shadow_half[1], GX_GYZ),
            by_axis(shadow_second[0], GX_GYZ),
            by_axis(shadow_second[1], GX_GYZ),
        )
        cross_real, cross_imag, norm_second = (summed[0], summed[1], summed[2])
        omega_step = (cross_real / norm_second, cross_imag / norm_second)
        evolved = evolved + scale_complex(alpha_step, dir_hat) + scale_complex(omega_step, half_hat)
        residual = half_step - scale_complex(omega_step, second)
        if iteration + 1 < ITERS:
            along_second = times_complex(omega_step, (summed[5], summed[6]))
            rho_next = (summed[3] - along_second[0], summed[4] - along_second[1])
            beta_step = times_complex(
                divide_complex(rho_next, rho_now), divide_complex(alpha_step, omega_step)
            )
            direction = residual + scale_complex(
                beta_step, direction - scale_complex(omega_step, image)
            )
            rho_now = rho_next
    return (evolved, residual)


def solution(mesh):
    finer = Mesh(
        mesh.devices.reshape(mesh.shape["orb"], mesh.shape["gx"], 8, 2),
        ("orb", "gx", "gyz_0", "gyz_1"),
    )
    return jax.shard_map(
        shards,
        mesh=finer,
        in_specs=(P(None, "orb", "gx", GYZ, None), P("gx", GYZ, None)),
        out_specs=(P(None, "orb", "gx", GYZ, None), P(None, "orb", "gx", GYZ, None)),
        check_vma=False,
    )
```

profile of v0, /device:TPU:1, one launch (start us, length us, event | category | flops | bytes accessed | tf_op | source)
XLA Modules:
  0.0 460.2 jit_solution(8637743133134373983)
XLA Ops:
  2.8 4.6 %collective-permute-start.1 = (f32[2,3,2,8,128]{4,3,2,1,0:T(8,128)S(1)}, f32[2,3,2,8,128]{4,3,2,1,0:T(8,128)S(1)}, u32[]{:S(2)}, u32[]{:S(2)}) collective-permute-start(f32[2,3,2,8,128]{4,3,2,1,0:T(8,128)S(1)} %get-tuple-element.312), channel_id=1, source_target_pairs={{0,16},{16,32},{32,48},{48,64},{64,80},{80,96},{96,112},{1,17},{17... | collective-permute-start | bytes 147464 | tf_op jit(solution)/shard_map/ppermute | solution.py:25
  8.6 5.3 %collective-permute-start.3 = (f32[2,3,16,2,128]{4,3,2,1,0:T(2,128)S(1)}, f32[2,3,16,2,128]{4,3,2,1,0:T(2,128)S(1)}, u32[]{:S(2)}, u32[]{:S(2)}) collective-permute-start(f32[2,3,16,2,128]{4,3,2,1,0:T(2,128)S(1)} %get-tuple-element.309), channel_id=1, source_target_pairs={{0,1},{1,2},{2,3},{3,4},{4,5},{5,6},{6,7},{7,8},{8,9},{9,10},{10,1... | collective-permute-start | bytes 294920 | tf_op jit(solution)/shard_map/ppermute | solution.py:25
  13.9 4.7 %collective-permute-start.2 = (f32[2,3,16,2,128]{4,3,2,1,0:T(2,128)S(1)}, f32[2,3,16,2,128]{4,3,2,1,0:T(2,128)S(1)}, u32[]{:S(2)}, u32[]{:S(2)}) collective-permute-start(f32[2,3,16,2,128]{4,3,2,1,0:T(2,128)S(1)} %get-tuple-element.310), channel_id=1, source_target_pairs={{1,0},{2,1},{3,2},{4,3},{5,4},{6,5},{7,6},{8,7},{9,8},{10,9},{11,1... | collective-permute-start | bytes 294920 | tf_op jit(solution)/shard_map/ppermute | solution.py:26
  30.8 4.1 collective-permute-done.6
  37.0 14.2 %all-reduce.42 = (f32[3]{0:T(128)S(1)}, f32[3]{0:T(128)S(1)}, f32[3]{0:T(128)S(1)}, f32[3]{0:T(128)S(1)}) all-reduce(f32[3]{0:T(128)S(1)} %get-tuple-element.43, f32[3]{0:T(128)S(1)} %get-tuple-element.3, f32[3]{0:T(128)S(1)} %get-tuple-element.42, f32[3]{0:T(128)S(1)} %get-tuple-element.2), channel_id=1, replica_groups=mesh['orb'=4,'gx'=8,'gyz_0'=8,'gyz_1'=2] {'gx'}, use_global_device_ids=true, to_apply=%region_1.2 | all-reduce | flops 12 | bytes 96 | tf_op jit(solution)/shard_map/psum | solution.py:39
  51.3 17.8 %all-reduce.34 = (f32[3]{0:T(128)S(1)}, f32[3]{0:T(128)S(1)}, f32[3]{0:T(128)S(1)}, f32[3]{0:T(128)S(1)}) all-reduce(f32[3]{0:T(128)S(1)} %get-tuple-element.108, f32[3]{0:T(128)S(1)} %get-tuple-element.109, f32[3]{0:T(128)S(1)} %get-tuple-element.110, ...), channel_id=1, replica_groups=mesh['orb'=4,'gx'=8,'gyz_0'=8,'gyz_1'=2] {'gyz_0'}, use_global_device_ids=true, to_apply=%region_2.3 | all-reduce | flops 12 | bytes 96 | tf_op jit(solution)/shard_map/psum | solution.py:39
  69.1 8.8 %all-reduce.50 = (f32[3]{0:T(128)S(1)}, f32[3]{0:T(128)S(1)}, f32[3]{0:T(128)S(1)}, f32[3]{0:T(128)S(1)}) all-reduce(f32[3]{0:T(128)S(1)} %get-tuple-element.74, f32[3]{0:T(128)S(1)} %get-tuple-element.75, f32[3]{0:T(128)S(1)} %get-tuple-element.76, ...), channel_id=1, replica_groups=mesh['orb'=4,'gx'=8,'gyz_0'=8,'gyz_1'=2] {'gyz_1'}, use_global_device_ids=true, to_apply=%region_3.4 | all-reduce | flops 12 | bytes 96 | tf_op jit(solution)/shard_map/psum | solution.py:39
  93.6 14.2 %all-reduce.41 = (f32[3]{0:T(128)S(1)}, f32[3]{0:T(128)S(1)}, f32[3]{0:T(128)S(1)}, f32[3]{0:T(128)S(1)}, f32[3]{0:T(128)S(1)}, /*index=5*/f32[3]{0:T(128)S(1)}, f32[3]{0:T(128)S(1)}) all-reduce(f32[3]{0:T(128)S(1)} %get-tuple-element.40, f32[3]{0:T(128)S(1)} %fusion.80, ...), channel_id=1, replica_groups=mesh['orb'=4,'gx'=8,'gyz_0'=8,'gyz_1'=2] {'gx'}, use_global_device_ids=true, to_apply=%region_25.26 | all-reduce | flops 21 | bytes 168 | tf_op jit(solution)/shard_map/psum | solution.py:39
  107.8 13.0 %all-reduce.33 = (f32[3]{0:T(128)S(1)}, f32[3]{0:T(128)S(1)}, f32[3]{0:T(128)S(1)}, f32[3]{0:T(128)S(1)}, f32[3]{0:T(128)S(1)}, /*index=5*/f32[3]{0:T(128)S(1)}, f32[3]{0:T(128)S(1)}) all-reduce(f32[3]{0:T(128)S(1)} %get-tuple-element.101, ...), channel_id=1, replica_groups=mesh['orb'=4,'gx'=8,'gyz_0'=8,'gyz_1'=2] {'gyz_0'}, use_global_device_ids=true, to_apply=%region_26.27 | all-reduce | flops 21 | bytes 168 | tf_op jit(solution)/shard_map/psum | solution.py:39
  120.8 8.4 %all-reduce.49 = (f32[3]{0:T(128)S(1)}, f32[3]{0:T(128)S(1)}, f32[3]{0:T(128)S(1)}, f32[3]{0:T(128)S(1)}, f32[3]{0:T(128)S(1)}, /*index=5*/f32[3]{0:T(128)S(1)}, f32[3]{0:T(128)S(1)}) all-reduce(f32[3]{0:T(128)S(1)} %get-tuple-element.67, f32[3]{0:T(128)S(1)} %get-tuple-element.68, ...), channel_id=1, replica_groups=mesh['orb'=4,'gx'=8,'gyz_0'=8,'gyz_1'=2] {'gyz_1'}, use_global_device_ids=true, to_apply=%region_27.28 | all-reduce | flops 21 | bytes 168 | tf_op jit(solution)/shard_map/psum | solution.py:39
  144.3 14.2 %all-reduce.40 = (f32[3]{0:T(128)S(1)}, f32[3]{0:T(128)S(1)}) all-reduce(f32[3]{0:T(128)S(1)} %get-tuple-element.23, f32[3]{0:T(128)S(1)} %get-tuple-element.22), channel_id=1, replica_groups=mesh['orb'=4,'gx'=8,'gyz_0'=8,'gyz_1'=2] {'gx'}, use_global_device_ids=true, to_apply=%region_49.50 | all-reduce | flops 6 | bytes 48 | tf_op jit(solution)/shard_map/psum | solution.py:39
  158.5 14.3 %all-reduce.32 = (f32[3]{0:T(128)S(1)}, f32[3]{0:T(128)S(1)}) all-reduce(f32[3]{0:T(128)S(1)} %get-tuple-element.99, f32[3]{0:T(128)S(1)} %get-tuple-element.100), channel_id=1, replica_groups=mesh['orb'=4,'gx'=8,'gyz_0'=8,'gyz_1'=2] {'gyz_0'}, use_global_device_ids=true, to_apply=%region_50.51 | all-reduce | flops 6 | bytes 48 | tf_op jit(solution)/shard_map/psum | solution.py:39
  172.8 7.4 %all-reduce.48 = (f32[3]{0:T(128)S(1)}, f32[3]{0:T(128)S(1)}) all-reduce(f32[3]{0:T(128)S(1)} %get-tuple-element.65, f32[3]{0:T(128)S(1)} %get-tuple-element.66), channel_id=1, replica_groups=mesh['orb'=4,'gx'=8,'gyz_0'=8,'gyz_1'=2] {'gyz_1'}, use_global_device_ids=true, to_apply=%region_51.52 | all-reduce | flops 6 | bytes 48 | tf_op jit(solution)/shard_map/psum | solution.py:39
  190.2 3.9 collective-permute-done.18
  197.1 14.7 %all-reduce.39 = (f32[3]{0:T(128)S(1)}, f32[3]{0:T(128)S(1)}, f32[3]{0:T(128)S(1)}, f32[3]{0:T(128)S(1)}, f32[3]{0:T(128)S(1)}, /*index=5*/f32[3]{0:T(128)S(1)}, f32[3]{0:T(128)S(1)}) all-reduce(f32[3]{0:T(128)} %get-tuple-element.36, f32[3]{0:T(128)S(1)} %fusion.81, ...), channel_id=1, replica_groups=mesh['orb'=4,'gx'=8,'gyz_0'=8,'gyz_1'=2] {'gx'}, use_global_device_ids=true, to_apply=%region_61.62 | all-reduce | flops 21 | bytes 168 | tf_op jit(solution)/shard_map/psum | solution.py:39
  211.7 12.8 %all-reduce.31 = (f32[3]{0:T(128)S(1)}, f32[3]{0:T(128)S(1)}, f32[3]{0:T(128)S(1)}, f32[3]{0:T(128)S(1)}, f32[3]{0:T(128)S(1)}, /*index=5*/f32[3]{0:T(128)S(1)}, f32[3]{0:T(128)S(1)}) all-reduce(f32[3]{0:T(128)S(1)} %get-tuple-element.92, f32[3]{0:T(128)S(1)} %get-tuple-element.93, ...), channel_id=1, replica_groups=mesh['orb'=4,'gx'=8,'gyz_0'=8,'gyz_1'=2] {'gyz_0'}, use_global_device_ids=true, to_apply=%region_62.63 | all-reduce | flops 21 | bytes 168 | tf_op jit(solution)/shard_map/psum | solution.py:39
  224.6 8.4 %all-reduce.47 = (f32[3]{0:T(128)S(1)}, f32[3]{0:T(128)S(1)}, f32[3]{0:T(128)S(1)}, f32[3]{0:T(128)S(1)}, f32[3]{0:T(128)S(1)}, /*index=5*/f32[3]{0:T(128)S(1)}, f32[3]{0:T(128)S(1)}) all-reduce(f32[3]{0:T(128)S(1)} %get-tuple-element.58, f32[3]{0:T(128)S(1)} %get-tuple-element.59, ...), channel_id=1, replica_groups=mesh['orb'=4,'gx'=8,'gyz_0'=8,'gyz_1'=2] {'gyz_1'}, use_global_device_ids=true, to_apply=%region_63.64 | all-reduce | flops 21 | bytes 168 | tf_op jit(solution)/shard_map/psum | solution.py:39
  245.7 3.7 collective-permute-done.22
  252.1 14.2 %all-reduce.38 = (f32[3]{0:T(128)S(1)}, f32[3]{0:T(128)S(1)}) all-reduce(f32[3]{0:T(128)S(1)} %get-tuple-element.15, f32[3]{0:T(128)S(1)} %get-tuple-element.14), channel_id=1, replica_groups=mesh['orb'=4,'gx'=8,'gyz_0'=8,'gyz_1'=2] {'gx'}, use_global_device_ids=true, to_apply=%region_85.86 | all-reduce | flops 6 | bytes 48 | tf_op jit(solution)/shard_map/psum | solution.py:39
  266.4 14.1 %all-reduce.30 = (f32[3]{0:T(128)S(1)}, f32[3]{0:T(128)S(1)}) all-reduce(f32[3]{0:T(128)S(1)} %get-tuple-element.90, f32[3]{0:T(128)S(1)} %get-tuple-element.91), channel_id=1, replica_groups=mesh['orb'=4,'gx'=8,'gyz_0'=8,'gyz_1'=2] {'gyz_0'}, use_global_device_ids=true, to_apply=%region_86.87 | all-reduce | flops 6 | bytes 48 | tf_op jit(solution)/shard_map/psum | solution.py:39
  280.4 7.5 %all-reduce.46 = (f32[3]{0:T(128)S(1)}, f32[3]{0:T(128)S(1)}) all-reduce(f32[3]{0:T(128)S(1)} %get-tuple-element.56, f32[3]{0:T(128)S(1)} %get-tuple-element.57), channel_id=1, replica_groups=mesh['orb'=4,'gx'=8,'gyz_0'=8,'gyz_1'=2] {'gyz_1'}, use_global_device_ids=true, to_apply=%region_87.88 | all-reduce | flops 6 | bytes 48 | tf_op jit(solution)/shard_map/psum | solution.py:39
  299.1 3.9 collective-permute-done.26
  306.6 15.2 %all-reduce.37 = (f32[3]{0:T(128)}, f32[3]{0:T(128)}, f32[3]{0:T(128)}, f32[3]{0:T(128)}, f32[3]{0:T(128)}, /*index=5*/f32[3]{0:T(128)}, f32[3]{0:T(128)}) all-reduce(f32[3]{0:T(128)} %get-tuple-element.32, f32[3]{0:T(128)} %fusion.82, f32[3]{0:T(128)} %get-tuple-element.33, ...), channel_id=1, replica_groups=mesh['orb'=4,'gx'=8,'gyz_0'=8,'gyz_1'=2] {'gx'}, use_global_device_ids=true, to_apply=%region_97.98 | all-reduce | flops 21 | bytes 168 | tf_op jit(solution)/shard_map/psum | solution.py:39
  321.8 13.9 %all-reduce.29 = (f32[3]{0:T(128)}, f32[3]{0:T(128)}, f32[3]{0:T(128)}, f32[3]{0:T(128)}, f32[3]{0:T(128)}, /*index=5*/f32[3]{0:T(128)}, f32[3]{0:T(128)}) all-reduce(f32[3]{0:T(128)} %get-tuple-element.83, f32[3]{0:T(128)} %get-tuple-element.84, ...), channel_id=1, replica_groups=mesh['orb'=4,'gx'=8,'gyz_0'=8,'gyz_1'=2] {'gyz_0'}, use_global_device_ids=true, to_apply=%region_98.99 | all-reduce | flops 21 | bytes 168 | tf_op jit(solution)/shard_map/psum | solution.py:39
  335.7 8.8 %all-reduce.45 = (f32[3]{0:T(128)}, f32[3]{0:T(128)}, f32[3]{0:T(128)}, f32[3]{0:T(128)}, f32[3]{0:T(128)}, /*index=5*/f32[3]{0:T(128)}, f32[3]{0:T(128)}) all-reduce(f32[3]{0:T(128)} %get-tuple-element.49, f32[3]{0:T(128)} %get-tuple-element.50, ...), channel_id=1, replica_groups=mesh['orb'=4,'gx'=8,'gyz_0'=8,'gyz_1'=2] {'gyz_1'}, use_global_device_ids=true, to_apply=%region_99.100 | all-reduce | flops 21 | bytes 168 | tf_op jit(solution)/shard_map/psum | solution.py:39
  363.5 14.2 %all-reduce.36 = (f32[3]{0:T(128)S(1)}, f32[3]{0:T(128)S(1)}) all-reduce(f32[3]{0:T(128)S(1)} %get-tuple-element.7, f32[3]{0:T(128)S(1)} %get-tuple-element.6), channel_id=1, replica_groups=mesh['orb'=4,'gx'=8,'gyz_0'=8,'gyz_1'=2] {'gx'}, use_global_device_ids=true, to_apply=%region_121.122 | all-reduce | flops 6 | bytes 48 | tf_op jit(solution)/shard_map/psum | solution.py:39
  377.7 14.1 %all-reduce.28 = (f32[3]{0:T(128)S(1)}, f32[3]{0:T(128)S(1)}) all-reduce(f32[3]{0:T(128)S(1)} %get-tuple-element.81, f32[3]{0:T(128)S(1)} %get-tuple-element.82), channel_id=1, replica_groups=mesh['orb'=4,'gx'=8,'gyz_0'=8,'gyz_1'=2] {'gyz_0'}, use_global_device_ids=true, to_apply=%region_122.123 | all-reduce | flops 6 | bytes 48 | tf_op jit(solution)/shard_map/psum | solution.py:39
  391.8 7.5 %all-reduce.44 = (f32[3]{0:T(128)S(1)}, f32[3]{0:T(128)S(1)}) all-reduce(f32[3]{0:T(128)S(1)} %get-tuple-element.47, f32[3]{0:T(128)S(1)} %get-tuple-element.48), channel_id=1, replica_groups=mesh['orb'=4,'gx'=8,'gyz_0'=8,'gyz_1'=2] {'gyz_1'}, use_global_device_ids=true, to_apply=%region_123.124 | all-reduce | flops 6 | bytes 48 | tf_op jit(solution)/shard_map/psum | solution.py:39
  411.7 3.9 collective-permute-done.34
  418.4 15.1 %all-reduce.35 = (f32[3]{0:T(128)S(1)}, f32[3]{0:T(128)}, f32[3]{0:T(128)}) all-reduce(f32[3]{0:T(128)S(1)} %get-tuple-element.5, f32[3]{0:T(128)S(1)} %fusion.83, f32[3]{0:T(128)S(1)} %get-tuple-element.4), channel_id=1, replica_groups=mesh['orb'=4,'gx'=8,'gyz_0'=8,'gyz_1'=2] {'gx'}, use_global_device_ids=true, to_apply=%region_133.134 | all-reduce | flops 9 | bytes 72 | tf_op jit(solution)/shard_map/psum | solution.py:39
  433.5 13.9 %all-reduce.27 = (f32[3]{0:T(128)}, f32[3]{0:T(128)}, f32[3]{0:T(128)}) all-reduce(f32[3]{0:T(128)S(1)} %get-tuple-element.78, f32[3]{0:T(128)} %get-tuple-element.79, f32[3]{0:T(128)} %get-tuple-element.80), channel_id=1, replica_groups=mesh['orb'=4,'gx'=8,'gyz_0'=8,'gyz_1'=2] {'gyz_0'}, use_global_device_ids=true, to_apply=%region_134.135 | all-reduce | flops 9 | bytes 72 | tf_op jit(solution)/shard_map/psum | solution.py:39
  447.4 8.2 %all-reduce.43 = (f32[3]{0:T(128)S(1)}, f32[3]{0:T(128)S(1)}, f32[3]{0:T(128)S(1)}) all-reduce(f32[3]{0:T(128)} %get-tuple-element.44, f32[3]{0:T(128)} %get-tuple-element.45, f32[3]{0:T(128)} %get-tuple-element.46), channel_id=1, replica_groups=mesh['orb'=4,'gx'=8,'gyz_0'=8,'gyz_1'=2] {'gyz_1'}, use_global_device_ids=true, to_apply=%region_135.136 | all-reduce | flops 9 | bytes 72 | tf_op jit(solution)/shard_map/psum | solution.py:39
  (289 shorter events, 129.2 us)
Async XLA Ops:
  1.5 19.1 %collective-permute-start = (f32[2,3,2,8,128]{4,3,2,1,0:T(8,128)S(1)}, f32[2,3,2,8,128]{4,3,2,1,0:T(8,128)S(1)}, u32[]{:S(2)}, u32[]{:S(2)}) collective-permute-start(f32[2,3,2,8,128]{4,3,2,1,0:T(8,128)S(1)} %get-tuple-element.311), channel_id=1, source_target_pairs={{16,0},{32,16},{48,32},{64,48},{80,64},{96,80},{112,96},{17,1},{33... | collective-permute-start | bytes 147464 | tf_op jit(solution)/shard_map/ppermute | solution.py:26
  2.8 16.7 %collective-permute-start.1 = (f32[2,3,2,8,128]{4,3,2,1,0:T(8,128)S(1)}, f32[2,3,2,8,128]{4,3,2,1,0:T(8,128)S(1)}, u32[]{:S(2)}, u32[]{:S(2)}) collective-permute-start(f32[2,3,2,8,128]{4,3,2,1,0:T(8,128)S(1)} %get-tuple-element.312), channel_id=1, source_target_pairs={{0,16},{16,32},{32,48},{48,64},{64,80},{80,96},{96,112},{1,17},{17... | collective-permute-start | bytes 147464 | tf_op jit(solution)/shard_map/ppermute | solution.py:25
  8.6 12.0 %collective-permute-start.3 = (f32[2,3,16,2,128]{4,3,2,1,0:T(2,128)S(1)}, f32[2,3,16,2,128]{4,3,2,1,0:T(2,128)S(1)}, u32[]{:S(2)}, u32[]{:S(2)}) collective-permute-start(f32[2,3,16,2,128]{4,3,2,1,0:T(2,128)S(1)} %get-tuple-element.309), channel_id=1, source_target_pairs={{0,1},{1,2},{2,3},{3,4},{4,5},{5,6},{6,7},{7,8},{8,9},{9,10},{10,1... | collective-permute-start | bytes 294920 | tf_op jit(solution)/shard_map/ppermute | solution.py:25
  13.9 6.8 %collective-permute-start.2 = (f32[2,3,16,2,128]{4,3,2,1,0:T(2,128)S(1)}, f32[2,3,16,2,128]{4,3,2,1,0:T(2,128)S(1)}, u32[]{:S(2)}, u32[]{:S(2)}) collective-permute-start(f32[2,3,16,2,128]{4,3,2,1,0:T(2,128)S(1)} %get-tuple-element.310), channel_id=1, source_target_pairs={{1,0},{2,1},{3,2},{4,3},{5,4},{6,5},{7,6},{8,7},{9,8},{10,9},{11,1... | collective-permute-start | bytes 294920 | tf_op jit(solution)/shard_map/ppermute | solution.py:26
  22.6 8.1 %collective-permute-start.5 = (f32[2,3,2,8,128]{4,3,2,1,0:T(8,128)S(1)}, f32[2,3,2,8,128]{4,3,2,1,0:T(8,128)S(1)}, u32[]{:S(2)}, u32[]{:S(2)}) collective-permute-start(f32[2,3,2,8,128]{4,3,2,1,0:T(8,128)S(1)} %get-tuple-element.302), channel_id=1, source_target_pairs={{0,16},{16,32},{32,48},{48,64},{64,80},{80,96},{96,112},{1,17},{17... | collective-permute-start | bytes 147464 | tf_op jit(solution)/shard_map/ppermute | solution.py:25
  25.0 5.7 %collective-permute-start.4 = (f32[2,3,2,8,128]{4,3,2,1,0:T(8,128)S(1)}, f32[2,3,2,8,128]{4,3,2,1,0:T(8,128)S(1)}, u32[]{:S(2)}, u32[]{:S(2)}) collective-permute-start(f32[2,3,2,8,128]{4,3,2,1,0:T(8,128)S(1)} %get-tuple-element.303), channel_id=1, source_target_pairs={{16,0},{32,16},{48,32},{64,48},{80,64},{96,80},{112,96},{17,1},{33... | collective-permute-start | bytes 147464 | tf_op jit(solution)/shard_map/ppermute | solution.py:26
  28.4 6.5 %collective-permute-start.6 = (f32[2,3,16,2,128]{4,3,2,1,0:T(2,128)S(1)}, f32[2,3,16,2,128]{4,3,2,1,0:T(2,128)S(1)}, u32[]{:S(2)}, u32[]{:S(2)}) collective-permute-start(f32[2,3,16,2,128]{4,3,2,1,0:T(2,128)S(1)} %get-tuple-element.305), channel_id=1, source_target_pairs={{1,0},{2,1},{3,2},{4,3},{5,4},{6,5},{7,6},{8,7},{9,8},{10,9},{11,1... | collective-permute-start | bytes 294920 | tf_op jit(solution)/shard_map/ppermute | solution.py:26
  79.0 8.7 %collective-permute-start.9 = (f32[2,3,2,8,128]{4,3,2,1,0:T(8,128)S(1)}, f32[2,3,2,8,128]{4,3,2,1,0:T(8,128)S(1)}, u32[]{:S(2)}, u32[]{:S(2)}) collective-permute-start(f32[2,3,2,8,128]{4,3,2,1,0:T(8,128)S(1)} %get-tuple-element.294), channel_id=1, source_target_pairs={{0,16},{16,32},{32,48},{48,64},{64,80},{80,96},{96,112},{1,17},{17... | collective-permute-start | bytes 147464 | tf_op jit(solution)/shard_map/ppermute | solution.py:25
  81.9 5.7 %collective-permute-start.8 = (f32[2,3,2,8,128]{4,3,2,1,0:T(8,128)S(1)}, f32[2,3,2,8,128]{4,3,2,1,0:T(8,128)S(1)}, u32[]{:S(2)}, u32[]{:S(2)}) collective-permute-start(f32[2,3,2,8,128]{4,3,2,1,0:T(8,128)S(1)} %get-tuple-element.295), channel_id=1, source_target_pairs={{16,0},{32,16},{48,32},{64,48},{80,64},{96,80},{112,96},{17,1},{33... | collective-permute-start | bytes 147464 | tf_op jit(solution)/shard_map/ppermute | solution.py:26
  85.2 5.9 %collective-permute-start.10 = (f32[2,3,16,2,128]{4,3,2,1,0:T(2,128)S(1)}, f32[2,3,16,2,128]{4,3,2,1,0:T(2,128)S(1)}, u32[]{:S(2)}, u32[]{:S(2)}) collective-permute-start(f32[2,3,16,2,128]{4,3,2,1,0:T(2,128)S(1)} %get-tuple-element.297), channel_id=1, source_target_pairs={{1,0},{2,1},{3,2},{4,3},{5,4},{6,5},{7,6},{8,7},{9,8},{10,9},{11,1... | collective-permute-start | bytes 294920 | tf_op jit(solution)/shard_map/ppermute | solution.py:26
  130.6 7.8 %collective-permute-start.13 = (f32[2,3,2,8,128]{4,3,2,1,0:T(8,128)S(1)}, f32[2,3,2,8,128]{4,3,2,1,0:T(8,128)S(1)}, u32[]{:S(2)}, u32[]{:S(2)}) collective-permute-start(f32[2,3,2,8,128]{4,3,2,1,0:T(8,128)S(1)} %get-tuple-element.286), channel_id=1, source_target_pairs={{0,16},{16,32},{32,48},{48,64},{64,80},{80,96},{96,112},{1,17},{17... | collective-permute-start | bytes 147464 | tf_op jit(solution)/shard_map/ppermute | solution.py:25
  132.7 5.7 %collective-permute-start.12 = (f32[2,3,2,8,128]{4,3,2,1,0:T(8,128)S(1)}, f32[2,3,2,8,128]{4,3,2,1,0:T(8,128)S(1)}, u32[]{:S(2)}, u32[]{:S(2)}) collective-permute-start(f32[2,3,2,8,128]{4,3,2,1,0:T(8,128)S(1)} %get-tuple-element.287), channel_id=1, source_target_pairs={{16,0},{32,16},{48,32},{64,48},{80,64},{96,80},{112,96},{17,1},{33... | collective-permute-start | bytes 147464 | tf_op jit(solution)/shard_map/ppermute | solution.py:26
  136.3 5.9 %collective-permute-start.14 = (f32[2,3,16,2,128]{4,3,2,1,0:T(2,128)S(1)}, f32[2,3,16,2,128]{4,3,2,1,0:T(2,128)S(1)}, u32[]{:S(2)}, u32[]{:S(2)}) collective-permute-start(f32[2,3,16,2,128]{4,3,2,1,0:T(2,128)S(1)} %get-tuple-element.289), channel_id=1, source_target_pairs={{1,0},{2,1},{3,2},{4,3},{5,4},{6,5},{7,6},{8,7},{9,8},{10,9},{11,1... | collective-permute-start | bytes 294920 | tf_op jit(solution)/shard_map/ppermute | solution.py:26
  181.9 8.2 %collective-permute-start.17 = (f32[2,3,2,8,128]{4,3,2,1,0:T(8,128)S(1)}, f32[2,3,2,8,128]{4,3,2,1,0:T(8,128)S(1)}, u32[]{:S(2)}, u32[]{:S(2)}) collective-permute-start(f32[2,3,2,8,128]{4,3,2,1,0:T(8,128)S(1)} %get-tuple-element.280), channel_id=1, source_target_pairs={{0,16},{16,32},{32,48},{48,64},{64,80},{80,96},{96,112},{1,17},{17... | collective-permute-start | bytes 147464 | tf_op jit(solution)/shard_map/ppermute | solution.py:25
  183.8 6.2 %collective-permute-start.16 = (f32[2,3,2,8,128]{4,3,2,1,0:T(8,128)S(1)}, f32[2,3,2,8,128]{4,3,2,1,0:T(8,128)S(1)}, u32[]{:S(2)}, u32[]{:S(2)}) collective-permute-start(f32[2,3,2,8,128]{4,3,2,1,0:T(8,128)S(1)} %get-tuple-element.281), channel_id=1, source_target_pairs={{16,0},{32,16},{48,32},{64,48},{80,64},{96,80},{112,96},{17,1},{33... | collective-permute-start | bytes 147464 | tf_op jit(solution)/shard_map/ppermute | solution.py:26
  185.2 5.0 %collective-permute-start.19 = (f32[2,3,16,2,128]{4,3,2,1,0:T(2,128)S(1)}, f32[2,3,16,2,128]{4,3,2,1,0:T(2,128)S(1)}, u32[]{:S(2)}, u32[]{:S(2)}) collective-permute-start(f32[2,3,16,2,128]{4,3,2,1,0:T(2,128)S(1)} %get-tuple-element.282), channel_id=1, source_target_pairs={{0,1},{1,2},{2,3},{3,4},{4,5},{5,6},{6,7},{7,8},{8,9},{9,10},{10,1... | collective-permute-start | bytes 294920 | tf_op jit(solution)/shard_map/ppermute | solution.py:25
  188.1 5.9 %collective-permute-start.18 = (f32[2,3,16,2,128]{4,3,2,1,0:T(2,128)S(1)}, f32[2,3,16,2,128]{4,3,2,1,0:T(2,128)S(1)}, u32[]{:S(2)}, u32[]{:S(2)}) collective-permute-start(f32[2,3,16,2,128]{4,3,2,1,0:T(2,128)S(1)} %get-tuple-element.283), channel_id=1, source_target_pairs={{1,0},{2,1},{3,2},{4,3},{5,4},{6,5},{7,6},{8,7},{9,8},{10,9},{11,1... | collective-permute-start | bytes 294920 | tf_op jit(solution)/shard_map/ppermute | solution.py:26
  237.8 7.8 %collective-permute-start.21 = (f32[2,3,2,8,128]{4,3,2,1,0:T(8,128)S(1)}, f32[2,3,2,8,128]{4,3,2,1,0:T(8,128)S(1)}, u32[]{:S(2)}, u32[]{:S(2)}) collective-permute-start(f32[2,3,2,8,128]{4,3,2,1,0:T(8,128)S(1)} %get-tuple-element.272), channel_id=1, source_target_pairs={{0,16},{16,32},{32,48},{48,64},{64,80},{80,96},{96,112},{1,17},{17... | collective-permute-start | bytes 147464 | tf_op jit(solution)/shard_map/ppermute | solution.py:25
  239.8 5.7 %collective-permute-start.20 = (f32[2,3,2,8,128]{4,3,2,1,0:T(8,128)S(1)}, f32[2,3,2,8,128]{4,3,2,1,0:T(8,128)S(1)}, u32[]{:S(2)}, u32[]{:S(2)}) collective-permute-start(f32[2,3,2,8,128]{4,3,2,1,0:T(8,128)S(1)} %get-tuple-element.273), channel_id=1, source_target_pairs={{16,0},{32,16},{48,32},{64,48},{80,64},{96,80},{112,96},{17,1},{33... | collective-permute-start | bytes 147464 | tf_op jit(solution)/shard_map/ppermute | solution.py:26
  243.4 5.9 %collective-permute-start.22 = (f32[2,3,16,2,128]{4,3,2,1,0:T(2,128)S(1)}, f32[2,3,16,2,128]{4,3,2,1,0:T(2,128)S(1)}, u32[]{:S(2)}, u32[]{:S(2)}) collective-permute-start(f32[2,3,16,2,128]{4,3,2,1,0:T(2,128)S(1)} %get-tuple-element.275), channel_id=1, source_target_pairs={{1,0},{2,1},{3,2},{4,3},{5,4},{6,5},{7,6},{8,7},{9,8},{10,9},{11,1... | collective-permute-start | bytes 294920 | tf_op jit(solution)/shard_map/ppermute | solution.py:26
  290.8 8.2 %collective-permute-start.25 = (f32[2,3,2,8,128]{4,3,2,1,0:T(8,128)S(1)}, f32[2,3,2,8,128]{4,3,2,1,0:T(8,128)S(1)}, u32[]{:S(2)}, u32[]{:S(2)}) collective-permute-start(f32[2,3,2,8,128]{4,3,2,1,0:T(8,128)S(1)} %get-tuple-element.266), channel_id=1, source_target_pairs={{0,16},{16,32},{32,48},{48,64},{64,80},{80,96},{96,112},{1,17},{17... | collective-permute-start | bytes 147464 | tf_op jit(solution)/shard_map/ppermute | solution.py:25
  292.7 6.2 %collective-permute-start.24 = (f32[2,3,2,8,128]{4,3,2,1,0:T(8,128)S(1)}, f32[2,3,2,8,128]{4,3,2,1,0:T(8,128)S(1)}, u32[]{:S(2)}, u32[]{:S(2)}) collective-permute-start(f32[2,3,2,8,128]{4,3,2,1,0:T(8,128)S(1)} %get-tuple-element.267), channel_id=1, source_target_pairs={{16,0},{32,16},{48,32},{64,48},{80,64},{96,80},{112,96},{17,1},{33... | collective-permute-start | bytes 147464 | tf_op jit(solution)/shard_map/ppermute | solution.py:26
  294.1 4.9 %collective-permute-start.27 = (f32[2,3,16,2,128]{4,3,2,1,0:T(2,128)S(1)}, f32[2,3,16,2,128]{4,3,2,1,0:T(2,128)S(1)}, u32[]{:S(2)}, u32[]{:S(2)}) collective-permute-start(f32[2,3,16,2,128]{4,3,2,1,0:T(2,128)S(1)} %get-tuple-element.268), channel_id=1, source_target_pairs={{0,1},{1,2},{2,3},{3,4},{4,5},{5,6},{6,7},{7,8},{8,9},{9,10},{10,1... | collective-permute-start | bytes 294920 | tf_op jit(solution)/shard_map/ppermute | solution.py:25
  297.0 5.9 %collective-permute-start.26 = (f32[2,3,16,2,128]{4,3,2,1,0:T(2,128)S(1)}, f32[2,3,16,2,128]{4,3,2,1,0:T(2,128)S(1)}, u32[]{:S(2)}, u32[]{:S(2)}) collective-permute-start(f32[2,3,16,2,128]{4,3,2,1,0:T(2,128)S(1)} %get-tuple-element.269), channel_id=1, source_target_pairs={{1,0},{2,1},{3,2},{4,3},{5,4},{6,5},{7,6},{8,7},{9,8},{10,9},{11,1... | collective-permute-start | bytes 294920 | tf_op jit(solution)/shard_map/ppermute | solution.py:26
  349.4 8.0 %collective-permute-start.29 = (f32[2,3,2,8,128]{4,3,2,1,0:T(8,128)S(1)}, f32[2,3,2,8,128]{4,3,2,1,0:T(8,128)S(1)}, u32[]{:S(2)}, u32[]{:S(2)}) collective-permute-start(f32[2,3,2,8,128]{4,3,2,1,0:T(8,128)S(1)} %get-tuple-element.258), channel_id=1, source_target_pairs={{0,16},{16,32},{32,48},{48,64},{64,80},{80,96},{96,112},{1,17},{17... | collective-permute-start | bytes 147464 | tf_op jit(solution)/shard_map/ppermute | solution.py:25
  351.4 5.9 %collective-permute-start.28 = (f32[2,3,2,8,128]{4,3,2,1,0:T(8,128)S(1)}, f32[2,3,2,8,128]{4,3,2,1,0:T(8,128)S(1)}, u32[]{:S(2)}, u32[]{:S(2)}) collective-permute-start(f32[2,3,2,8,128]{4,3,2,1,0:T(8,128)S(1)} %get-tuple-element.259), channel_id=1, source_target_pairs={{16,0},{32,16},{48,32},{64,48},{80,64},{96,80},{112,96},{17,1},{33... | collective-permute-start | bytes 147464 | tf_op jit(solution)/shard_map/ppermute | solution.py:26
  352.8 4.7 %collective-permute-start.31 = (f32[2,3,16,2,128]{4,3,2,1,0:T(2,128)S(1)}, f32[2,3,16,2,128]{4,3,2,1,0:T(2,128)S(1)}, u32[]{:S(2)}, u32[]{:S(2)}) collective-permute-start(f32[2,3,16,2,128]{4,3,2,1,0:T(2,128)S(1)} %get-tuple-element.260), channel_id=1, source_target_pairs={{0,1},{1,2},{2,3},{3,4},{4,5},{5,6},{6,7},{7,8},{8,9},{9,10},{10,1... | collective-permute-start | bytes 294920 | tf_op jit(solution)/shard_map/ppermute | solution.py:25
  355.0 5.9 %collective-permute-start.30 = (f32[2,3,16,2,128]{4,3,2,1,0:T(2,128)S(1)}, f32[2,3,16,2,128]{4,3,2,1,0:T(2,128)S(1)}, u32[]{:S(2)}, u32[]{:S(2)}) collective-permute-start(f32[2,3,16,2,128]{4,3,2,1,0:T(2,128)S(1)} %get-tuple-element.261), channel_id=1, source_target_pairs={{1,0},{2,1},{3,2},{4,3},{5,4},{6,5},{7,6},{8,7},{9,8},{10,9},{11,1... | collective-permute-start | bytes 294920 | tf_op jit(solution)/shard_map/ppermute | solution.py:26
  403.3 8.2 %collective-permute-start.33 = (f32[2,3,2,8,128]{4,3,2,1,0:T(8,128)S(1)}, f32[2,3,2,8,128]{4,3,2,1,0:T(8,128)S(1)}, u32[]{:S(2)}, u32[]{:S(2)}) collective-permute-start(f32[2,3,2,8,128]{4,3,2,1,0:T(8,128)S(1)} %get-tuple-element.252), channel_id=1, source_target_pairs={{0,16},{16,32},{32,48},{48,64},{64,80},{80,96},{96,112},{1,17},{17... | collective-permute-start | bytes 147464 | tf_op jit(solution)/shard_map/ppermute | solution.py:25
  405.3 6.2 %collective-permute-start.32 = (f32[2,3,2,8,128]{4,3,2,1,0:T(8,128)S(1)}, f32[2,3,2,8,128]{4,3,2,1,0:T(8,128)S(1)}, u32[]{:S(2)}, u32[]{:S(2)}) collective-permute-start(f32[2,3,2,8,128]{4,3,2,1,0:T(8,128)S(1)} %get-tuple-element.253), channel_id=1, source_target_pairs={{16,0},{32,16},{48,32},{64,48},{80,64},{96,80},{112,96},{17,1},{33... | collective-permute-start | bytes 147464 | tf_op jit(solution)/shard_map/ppermute | solution.py:26
  406.7 4.9 %collective-permute-start.35 = (f32[2,3,16,2,128]{4,3,2,1,0:T(2,128)S(1)}, f32[2,3,16,2,128]{4,3,2,1,0:T(2,128)S(1)}, u32[]{:S(2)}, u32[]{:S(2)}) collective-permute-start(f32[2,3,16,2,128]{4,3,2,1,0:T(2,128)S(1)} %get-tuple-element.254), channel_id=1, source_target_pairs={{0,1},{1,2},{2,3},{3,4},{4,5},{5,6},{6,7},{7,8},{8,9},{9,10},{10,1... | collective-permute-start | bytes 294920 | tf_op jit(solution)/shard_map/ppermute | solution.py:25
  409.6 5.9 %collective-permute-start.34 = (f32[2,3,16,2,128]{4,3,2,1,0:T(2,128)S(1)}, f32[2,3,16,2,128]{4,3,2,1,0:T(2,128)S(1)}, u32[]{:S(2)}, u32[]{:S(2)}) collective-permute-start(f32[2,3,16,2,128]{4,3,2,1,0:T(2,128)S(1)} %get-tuple-element.255), channel_id=1, source_target_pairs={{1,0},{2,1},{3,2},{4,3},{5,4},{6,5},{7,6},{8,7},{9,8},{10,9},{11,1... | collective-permute-start | bytes 294920 | tf_op jit(solution)/shard_map/ppermute | solution.py:26
  (50 other events, 386.7 us)
where the time goes:
time: 462 us; the launch traced here: 460 us
  blocking collectives  295 us (64%)
  starting transfers between devices  79.9 us (17%)
  other arithmetic  44.2 us (10%)
  waiting for transfers between devices  29.9 us (6%)
  local copies, waits for them, and re-layouts  9.09 us (2%)
    psum x24, blocking collectives, by_axis(): array = lax.psum(array, axis)  295 us
    ppermute x18, starting transfers between devices, padded_2(): lax.ppermute(last, axis, up)  46.7 us
    ppermute x18, starting transfers between devices, padded_2(): lax.ppermute(leading, axis, [(b, a) for a, b in up])  33.3 us
    ppermute x18, waiting for transfers between devices, padded_2(): lax.ppermute(leading, axis, [(b, a) for a, b in up])  29.8 us
    sub x11, other arithmetic, scale_complex(): real_coef * vector[0] - imag_coef * vector[1]  12.4 us
    concatenate x17, other arithmetic, padded_2(): jnp.concatenate([jnp.pad(low, around), array, jnp.pad(high, around)], axi...  10.3 us
  transfers between devices with their start and end apart: 36, of which 8 were waited for; matrix products, arithmetic and copies ran while one was open for 1% of the time, Pallas kernels for 0%

commit v1 on v0

--- a/solution.py
+++ b/solution.py
@@ -36,7 +36,7 @@
 
 def by_axis(array, axes):
     for axis in axes:
-        array = lax.psum(array, axis)
+        array = jnp.sum(lax.all_gather(array, axis), axis=0)
     return array
 
 

time: 462 us -> 572 us (1.24); the launches traced: 460 us -> 563 us
  local copies, waits for them, and re-layouts: 9.09 us -> 86.7 us
  starting transfers between devices: 79.9 us -> 101 us
  other arithmetic: 44.2 us -> 63.1 us
  waiting for transfers between devices: 29.9 us -> 11.2 us
    unnamed x0 -> x24, blocking collectives: none -> 296 us
    psum x24 -> x0, blocking collectives: 295 us -> none  [by_axis(): array = lax.psum(array, axis)]
    unnamed x94 -> x299, local copies, waits for them, and re-layouts: 6.3 us -> 62.9 us
    ppermute x18, waiting for transfers between devices: 29.8 us -> 1.56 us  [padded_2(): lax.ppermute(leading, axis, [(b, a) for a, b in up])]
    all_gather x0 -> x102, local copies, waits for them, and re-layouts: none -> 21.1 us  [by_axis(): array = jnp.sum(lax.all_gather(array, axis), axis=0)]
    reduce_sum x0 -> x102, other arithmetic: none -> 15.9 us  [by_axis(): array = jnp.sum(lax.all_gather(array, axis), axis=0)]
    ppermute x18, starting transfers between devices: 46.7 us -> 58.7 us  [padded_2(): lax.ppermute(last, axis, up)]
    ppermute x18, waiting for transfers between devices: 0.05 us -> 9.61 us  [padded_2(): lax.ppermute(last, axis, up)]
  transfers between devices with their start and end apart: 36 -> 36, of which waited for: 8 -> 15; matrix products, arithmetic and copies ran while one was open for 1% -> 1% of each run, Pallas kernels for 0% -> 0%
where the time goes in v1:
time: 572 us; the launch traced here: 563 us
  blocking collectives  296 us (52%)
  starting transfers between devices  101 us (18%)
  local copies, waits for them, and re-layouts  86.7 us (15%)
  other arithmetic  63.1 us (11%)
  waiting for transfers between devices  11.2 us (2%)
    unnamed x24, blocking collectives  296 us
    unnamed x299, local copies, waits for them, and re-layouts  62.9 us
    ppermute x18, starting transfers between devices, padded_2(): lax.ppermute(last, axis, up)  58.7 us
    ppermute x18, starting transfers between devices, padded_2(): lax.ppermute(leading, axis, [(b, a) for a, b in up])  42.7 us
    all_gather x102, local copies, waits for them, and re-layouts, by_axis(): array = jnp.sum(lax.all_gather(array, axis), axis=0)  21.1 us
    reduce_sum x102, other arithmetic, by_axis(): array = jnp.sum(lax.all_gather(array, axis), axis=0)  15.9 us
    sub x11, other arithmetic, scale_complex(): real_coef * vector[0] - imag_coef * vector[1]  12.4 us
  transfers between devices with their start and end apart: 36, of which 15 were waited for; matrix products, arithmetic and copies ran while one was open for 1% of the time, Pallas kernels for 0%

profile of v1, /device:TPU:1, one launch (start us, length us, event | category | flops | bytes accessed | tf_op | source)
XLA Modules:
  0.0 562.6 jit_solution(7409381312549884526)
XLA Ops:
  1.8 8.7 %collective-permute-start.2 = (f32[2,3,16,2,128]{4,3,2,1,0:T(2,128)S(1)}, f32[2,3,16,2,128]{4,3,2,1,0:T(2,128)S(1)}, u32[]{:S(2)}, u32[]{:S(2)}) collective-permute-start(f32[2,3,16,2,128]{4,3,2,1,0:T(2,128)S(1)} %get-tuple-element.310), channel_id=1, source_target_pairs={{1,0},{2,1},{3,2},{4,3},{5,4},{6,5},{7,6},{8,7},{9,8},{10,9},{11,1... | collective-permute-start | bytes 294920 | tf_op jit(solution)/shard_map/ppermute | solution.py:26
  27.0 4.6 collective-permute-start.5
  41.8 14.0 %all-reduce.144 = (f32[24]{0:T(128)S(1)}, f32[24]{0:T(128)S(1)}, f32[24]{0:T(128)S(1)}, f32[24]{0:T(128)S(1)}) all-reduce(f32[24]{0:T(128)S(1)} %dynamic-update-slice, f32[24]{0:T(128)S(1)} %dynamic-update-slice.9, f32[24]{0:T(128)S(1)} %dynamic-update-slice.6, ...), channel_id=2, replica_groups=mesh['orb'=4,'gx'=8,'gyz_0'=8,'gyz_1'=2] {'gx'}, use_global_device_ids=true, to_apply=%add.27 | all-reduce | flops 96 | bytes 768
  57.2 16.6 %all-reduce.136 = (f32[24]{0:T(128)S(1)}, f32[24]{0:T(128)S(1)}, f32[24]{0:T(128)S(1)}, f32[24]{0:T(128)S(1)}) all-reduce(f32[24]{0:T(128)S(1)} %dynamic-update-slice.1, f32[24]{0:T(128)S(1)} %dynamic-update-slice.10, f32[24]{0:T(128)S(1)} %dynamic-update-slice.7, ...), channel_id=3, replica_groups=mesh['orb'=4,'gx'=8,'gyz_0'=8,'gyz_1'=2] {'gyz_0'}, use_global_device_ids=true, to_apply=%add.28 | all-reduce | flops 96 | bytes 768
  75.1 12.3 %all-reduce.152 = (f32[6]{0:T(128)S(1)}, f32[6]{0:T(128)S(1)}, f32[6]{0:T(128)S(1)}, f32[6]{0:T(128)S(1)}) all-reduce(f32[6]{0:T(128)S(1)} %dynamic-update-slice.2, f32[6]{0:T(128)S(1)} %dynamic-update-slice.11, f32[6]{0:T(128)S(1)} %dynamic-update-slice.8, ...), channel_id=4, replica_groups=mesh['orb'=4,'gx'=8,'gyz_0'=8,'gyz_1'=2] {'gyz_1'}, use_global_device_ids=true, to_apply=%add.29 | all-reduce | flops 24 | bytes 192
  90.2 4.0 collective-permute-start.9
  105.4 12.4 %all-reduce.143 = (f32[24]{0:T(128)S(1)}, f32[24]{0:T(128)S(1)}, f32[24]{0:T(128)S(1)}, f32[24]{0:T(128)S(1)}, f32[24]{0:T(128)S(1)}, /*index=5*/f32[24]{0:T(128)S(1)}, f32[24]{0:T(128)S(1)}) all-reduce(f32[24]{0:T(128)S(1)} %dynamic-update-slice.18, ...), channel_id=20, replica_groups=mesh['orb'=4,'gx'=8,'gyz_0'=8,'gyz_1'=2] {'gx'}, use_global_device_ids=true, to_apply=%add.45 | all-reduce | flops 168 | bytes 1344
  120.2 11.2 %all-reduce.135 = (f32[24]{0:T(128)S(1)}, f32[24]{0:T(128)S(1)}, f32[24]{0:T(128)S(1)}, f32[24]{0:T(128)S(1)}, f32[24]{0:T(128)S(1)}, /*index=5*/f32[24]{0:T(128)S(1)}, f32[24]{0:T(128)S(1)}) all-reduce(f32[24]{0:T(128)S(1)} %dynamic-update-slice.19, ...), channel_id=21, replica_groups=mesh['orb'=4,'gx'=8,'gyz_0'=8,'gyz_1'=2] {'gyz_0'}, use_global_device_ids=true, to_apply=%add.46 | all-reduce | flops 168 | bytes 1344
  133.8 11.3 %all-reduce.151 = (f32[6]{0:T(128)S(1)}, f32[6]{0:T(128)S(1)}, f32[6]{0:T(128)S(1)}, f32[6]{0:T(128)S(1)}, f32[6]{0:T(128)S(1)}, /*index=5*/f32[6]{0:T(128)S(1)}, f32[6]{0:T(128)S(1)}) all-reduce(f32[6]{0:T(128)S(1)} %dynamic-update-slice.20, ...), channel_id=22, replica_groups=mesh['orb'=4,'gx'=8,'gyz_0'=8,'gyz_1'=2] {'gyz_1'}, use_global_device_ids=true, to_apply=%add.47 | all-reduce | flops 42 | bytes 336
  149.2 4.0 collective-permute-start.13
  162.9 12.4 %all-reduce.142 = (f32[24]{0:T(128)S(1)}, f32[24]{0:T(128)S(1)}) all-reduce(f32[24]{0:T(128)S(1)} %dynamic-update-slice.36, f32[24]{0:T(128)S(1)} %dynamic-update-slice.33), channel_id=38, replica_groups=mesh['orb'=4,'gx'=8,'gyz_0'=8,'gyz_1'=2] {'gx'}, use_global_device_ids=true, to_apply=%add.63 | all-reduce | flops 48 | bytes 384
  176.0 12.5 %all-reduce.134 = (f32[24]{0:T(128)S(1)}, f32[24]{0:T(128)S(1)}) all-reduce(f32[24]{0:T(128)S(1)} %dynamic-update-slice.37, f32[24]{0:T(128)S(1)} %dynamic-update-slice.34), channel_id=39, replica_groups=mesh['orb'=4,'gx'=8,'gyz_0'=8,'gyz_1'=2] {'gyz_0'}, use_global_device_ids=true, to_apply=%add.64 | all-reduce | flops 48 | bytes 384
  189.2 10.8 %all-reduce.150 = (f32[6]{0:T(128)S(1)}, f32[6]{0:T(128)S(1)}) all-reduce(f32[6]{0:T(128)S(1)} %dynamic-update-slice.38, f32[6]{0:T(128)S(1)} %dynamic-update-slice.35), channel_id=40, replica_groups=mesh['orb'=4,'gx'=8,'gyz_0'=8,'gyz_1'=2] {'gyz_1'}, use_global_device_ids=true, to_apply=%add.65 | all-reduce | flops 12 | bytes 96
  203.2 4.0 collective-permute-start.17
  221.4 12.4 %all-reduce.141 = (f32[24]{0:T(128)S(1)}, f32[24]{0:T(128)S(1)}, f32[24]{0:T(128)S(1)}, f32[24]{0:T(128)S(1)}, f32[24]{0:T(128)S(1)}, /*index=5*/f32[24]{0:T(128)S(1)}, f32[24]{0:T(128)S(1)}) all-reduce(f32[24]{0:T(128)S(1)} %dynamic-update-slice.45, ...), channel_id=47, replica_groups=mesh['orb'=4,'gx'=8,'gyz_0'=8,'gyz_1'=2] {'gx'}, use_global_device_ids=true, to_apply=%add.72 | all-reduce | flops 168 | bytes 1344
  236.2 12.8 %all-reduce.133 = (f32[24]{0:T(128)S(1)}, f32[24]{0:T(128)S(1)}, f32[24]{0:T(128)S(1)}, f32[24]{0:T(128)S(1)}, f32[24]{0:T(128)S(1)}, /*index=5*/f32[24]{0:T(128)S(1)}, f32[24]{0:T(128)S(1)}) all-reduce(f32[24]{0:T(128)S(1)} %dynamic-update-slice.46, ...), channel_id=48, replica_groups=mesh['orb'=4,'gx'=8,'gyz_0'=8,'gyz_1'=2] {'gyz_0'}, use_global_device_ids=true, to_apply=%add.73 | all-reduce | flops 168 | bytes 1344
  251.5 10.9 %all-reduce.149 = (f32[6]{0:T(128)S(1)}, f32[6]{0:T(128)S(1)}, f32[6]{0:T(128)S(1)}, f32[6]{0:T(128)S(1)}, f32[6]{0:T(128)S(1)}, /*index=5*/f32[6]{0:T(128)S(1)}, f32[6]{0:T(128)S(1)}) all-reduce(f32[6]{0:T(128)S(1)} %dynamic-update-slice.47, ...), channel_id=49, replica_groups=mesh['orb'=4,'gx'=8,'gyz_0'=8,'gyz_1'=2] {'gyz_1'}, use_global_device_ids=true, to_apply=%add.74 | all-reduce | flops 42 | bytes 336
  269.2 4.0 collective-permute-start.21
  283.7 12.2 %all-reduce.140 = (f32[24]{0:T(128)S(1)}, f32[24]{0:T(128)S(1)}) all-reduce(f32[24]{0:T(128)S(1)} %dynamic-update-slice.63, f32[24]{0:T(128)S(1)} %dynamic-update-slice.60), channel_id=65, replica_groups=mesh['orb'=4,'gx'=8,'gyz_0'=8,'gyz_1'=2] {'gx'}, use_global_device_ids=true, to_apply=%add.90 | all-reduce | flops 48 | bytes 384
  296.5 12.9 %all-reduce.132 = (f32[24]{0:T(128)S(1)}, f32[24]{0:T(128)S(1)}) all-reduce(f32[24]{0:T(128)S(1)} %dynamic-update-slice.64, f32[24]{0:T(128)S(1)} %dynamic-update-slice.61), channel_id=66, replica_groups=mesh['orb'=4,'gx'=8,'gyz_0'=8,'gyz_1'=2] {'gyz_0'}, use_global_device_ids=true, to_apply=%add.91 | all-reduce | flops 48 | bytes 384
  310.1 10.8 %all-reduce.148 = (f32[6]{0:T(128)S(1)}, f32[6]{0:T(128)S(1)}) all-reduce(f32[6]{0:T(128)S(1)} %dynamic-update-slice.65, f32[6]{0:T(128)S(1)} %dynamic-update-slice.62), channel_id=67, replica_groups=mesh['orb'=4,'gx'=8,'gyz_0'=8,'gyz_1'=2] {'gyz_1'}, use_global_device_ids=true, to_apply=%add.92 | all-reduce | flops 12 | bytes 96
  325.3 4.0 collective-permute-start.25
  351.1 13.1 %all-reduce.139 = (f32[24]{0:T(128)}, f32[24]{0:T(128)}, f32[24]{0:T(128)S(1)}, f32[24]{0:T(128)S(1)}, f32[24]{0:T(128)S(1)}, /*index=5*/f32[24]{0:T(128)S(1)}, f32[24]{0:T(128)}) all-reduce(f32[24]{0:T(128)} %dynamic-update-slice.72, f32[24]{0:T(128)} %dynamic-update-slice.69, ...), channel_id=74, replica_groups=mesh['orb'=4,'gx'=8,'gyz_0'=8,'gyz_1'=2] {'gx'}, use_global_device_ids=true, to_apply=%add.99 | all-reduce | flops 168 | bytes 1344
  385.4 13.5 %all-reduce.131 = (f32[24]{0:T(128)}, f32[24]{0:T(128)}, f32[24]{0:T(128)S(1)}, f32[24]{0:T(128)S(1)}, f32[24]{0:T(128)S(1)}, /*index=5*/f32[24]{0:T(128)S(1)}, f32[24]{0:T(128)}) all-reduce(f32[24]{0:T(128)} %dynamic-update-slice.73, f32[24]{0:T(128)} %dynamic-update-slice.70, ...), channel_id=75, replica_groups=mesh['orb'=4,'gx'=8,'gyz_0'=8,'gyz_1'=2] {'gyz_0'}, use_global_device_ids=true, to_apply=%add.100 | all-reduce | flops 168 | bytes 1344
  416.9 11.6 %all-reduce.147 = (f32[6]{0:T(128)S(1)}, f32[6]{0:T(128)}, f32[6]{0:T(128)}, f32[6]{0:T(128)}, f32[6]{0:T(128)}, /*index=5*/f32[6]{0:T(128)}, f32[6]{0:T(128)S(1)}) all-reduce(f32[6]{0:T(128)} %dynamic-update-slice.74, f32[6]{0:T(128)} %dynamic-update-slice.71, ...), channel_id=76, replica_groups=mesh['orb'=4,'gx'=8,'gyz_0'=8,'gyz_1'=2] {'gyz_1'}, use_global_device_ids=true, to_apply=%add.101 | all-reduce | flops 42 | bytes 336
  460.5 12.2 %all-reduce.138 = (f32[24]{0:T(128)S(1)}, f32[24]{0:T(128)S(1)}) all-reduce(f32[24]{0:T(128)S(1)} %dynamic-update-slice.90, f32[24]{0:T(128)S(1)} %dynamic-update-slice.87), channel_id=92, replica_groups=mesh['orb'=4,'gx'=8,'gyz_0'=8,'gyz_1'=2] {'gx'}, use_global_device_ids=true, to_apply=%add.117 | all-reduce | flops 48 | bytes 384
  473.3 12.9 %all-reduce.130 = (f32[24]{0:T(128)S(1)}, f32[24]{0:T(128)S(1)}) all-reduce(f32[24]{0:T(128)S(1)} %dynamic-update-slice.91, f32[24]{0:T(128)S(1)} %dynamic-update-slice.88), channel_id=93, replica_groups=mesh['orb'=4,'gx'=8,'gyz_0'=8,'gyz_1'=2] {'gyz_0'}, use_global_device_ids=true, to_apply=%add.118 | all-reduce | flops 48 | bytes 384
  486.9 10.8 %all-reduce.146 = (f32[6]{0:T(128)S(1)}, f32[6]{0:T(128)S(1)}) all-reduce(f32[6]{0:T(128)S(1)} %dynamic-update-slice.92, f32[6]{0:T(128)S(1)} %dynamic-update-slice.89), channel_id=94, replica_groups=mesh['orb'=4,'gx'=8,'gyz_0'=8,'gyz_1'=2] {'gyz_1'}, use_global_device_ids=true, to_apply=%add.119 | all-reduce | flops 12 | bytes 96
  503.3 4.0 collective-permute-start.33
  519.3 12.4 %all-reduce.137 = (f32[24]{0:T(128)S(1)}, f32[24]{0:T(128)S(1)}, f32[24]{0:T(128)S(1)}) all-reduce(f32[24]{0:T(128)S(1)} %dynamic-update-slice.99, f32[24]{0:T(128)S(1)} %dynamic-update-slice.96, f32[24]{0:T(128)S(1)} %dynamic-update-slice.93), channel_id=101, replica_groups=mesh['orb'=4,'gx'=8,'gyz_0'=8,'gyz_1'=2] {'gx'}, use_global_device_ids=true, to_apply=%add.126 | all-reduce | flops 72 | bytes 576
  532.7 12.8 %all-reduce.129 = (f32[24]{0:T(128)S(1)}, f32[24]{0:T(128)S(1)}, f32[24]{0:T(128)S(1)}) all-reduce(f32[24]{0:T(128)S(1)} %dynamic-update-slice.100, f32[24]{0:T(128)S(1)} %dynamic-update-slice.97, f32[24]{0:T(128)S(1)} %dynamic-update-slice.94), channel_id=102, replica_groups=mesh['orb'=4,'gx'=8,'gyz_0'=8,'gyz_1'=2] {'gyz_0'}, use_global_device_ids=true, to_apply=%add.127 | all-reduce | flops 72 | bytes 576
  546.5 10.9 %all-reduce.145 = (f32[6]{0:T(128)S(1)}, f32[6]{0:T(128)S(1)}, f32[6]{0:T(128)S(1)}) all-reduce(f32[6]{0:T(128)S(1)} %dynamic-update-slice.101, f32[6]{0:T(128)S(1)} %dynamic-update-slice.98, f32[6]{0:T(128)S(1)} %dynamic-update-slice.95), channel_id=103, replica_groups=mesh['orb'=4,'gx'=8,'gyz_0'=8,'gyz_1'=2] {'gyz_1'}, use_global_device_ids=true, to_apply=%add.128 | all-reduce | flops 18 | bytes 144
  (698 shorter events, 225.1 us)
Async XLA Ops:
  1.8 21.9 %collective-permute-start.2 = (f32[2,3,16,2,128]{4,3,2,1,0:T(2,128)S(1)}, f32[2,3,16,2,128]{4,3,2,1,0:T(2,128)S(1)}, u32[]{:S(2)}, u32[]{:S(2)}) collective-permute-start(f32[2,3,16,2,128]{4,3,2,1,0:T(2,128)S(1)} %get-tuple-element.310), channel_id=1, source_target_pairs={{1,0},{2,1},{3,2},{4,3},{5,4},{6,5},{7,6},{8,7},{9,8},{10,9},{11,1... | collective-permute-start | bytes 294920 | tf_op jit(solution)/shard_map/ppermute | solution.py:26
  11.4 11.1 %collective-permute-start.1 = (f32[2,3,2,8,128]{4,3,2,1,0:T(8,128)S(1)}, f32[2,3,2,8,128]{4,3,2,1,0:T(8,128)S(1)}, u32[]{:S(2)}, u32[]{:S(2)}) collective-permute-start(f32[2,3,2,8,128]{4,3,2,1,0:T(8,128)S(1)} %get-tuple-element.312), channel_id=1, source_target_pairs={{0,16},{16,32},{32,48},{48,64},{64,80},{80,96},{96,112},{1,17},{17... | collective-permute-start | bytes 147464 | tf_op jit(solution)/shard_map/ppermute | solution.py:25
  12.7 11.0 %collective-permute-start = (f32[2,3,2,8,128]{4,3,2,1,0:T(8,128)S(1)}, f32[2,3,2,8,128]{4,3,2,1,0:T(8,128)S(1)}, u32[]{:S(2)}, u32[]{:S(2)}) collective-permute-start(f32[2,3,2,8,128]{4,3,2,1,0:T(8,128)S(1)} %get-tuple-element.311), channel_id=1, source_target_pairs={{16,0},{32,16},{48,32},{64,48},{80,64},{96,80},{112,96},{17,1},{33... | collective-permute-start | bytes 147464 | tf_op jit(solution)/shard_map/ppermute | solution.py:26
  14.0 9.8 %collective-permute-start.3 = (f32[2,3,16,2,128]{4,3,2,1,0:T(2,128)S(1)}, f32[2,3,16,2,128]{4,3,2,1,0:T(2,128)S(1)}, u32[]{:S(2)}, u32[]{:S(2)}) collective-permute-start(f32[2,3,16,2,128]{4,3,2,1,0:T(2,128)S(1)} %get-tuple-element.309), channel_id=1, source_target_pairs={{0,1},{1,2},{2,3},{3,4},{4,5},{5,6},{6,7},{7,8},{8,9},{9,10},{10,1... | collective-permute-start | bytes 294920 | tf_op jit(solution)/shard_map/ppermute | solution.py:25
  25.7 11.6 %collective-permute-start.4 = (f32[2,3,2,8,128]{4,3,2,1,0:T(8,128)S(1)}, f32[2,3,2,8,128]{4,3,2,1,0:T(8,128)S(1)}, u32[]{:S(2)}, u32[]{:S(2)}) collective-permute-start(f32[2,3,2,8,128]{4,3,2,1,0:T(8,128)S(1)} %get-tuple-element.303), channel_id=1, source_target_pairs={{16,0},{32,16},{48,32},{64,48},{80,64},{96,80},{112,96},{17,1},{33... | collective-permute-start | bytes 147464 | tf_op jit(solution)/shard_map/ppermute | solution.py:26
  27.0 10.3 %collective-permute-start.5 = (f32[2,3,2,8,128]{4,3,2,1,0:T(8,128)S(1)}, f32[2,3,2,8,128]{4,3,2,1,0:T(8,128)S(1)}, u32[]{:S(2)}, u32[]{:S(2)}) collective-permute-start(f32[2,3,2,8,128]{4,3,2,1,0:T(8,128)S(1)} %get-tuple-element.302), channel_id=1, source_target_pairs={{0,16},{16,32},{32,48},{48,64},{64,80},{80,96},{96,112},{1,17},{17... | collective-permute-start | bytes 147464 | tf_op jit(solution)/shard_map/ppermute | solution.py:25
  31.7 5.9 %collective-permute-start.6 = (f32[2,3,16,2,128]{4,3,2,1,0:T(2,128)S(1)}, f32[2,3,16,2,128]{4,3,2,1,0:T(2,128)S(1)}, u32[]{:S(2)}, u32[]{:S(2)}) collective-permute-start(f32[2,3,16,2,128]{4,3,2,1,0:T(2,128)S(1)} %get-tuple-element.305), channel_id=1, source_target_pairs={{1,0},{2,1},{3,2},{4,3},{5,4},{6,5},{7,6},{8,7},{9,8},{10,9},{11,1... | collective-permute-start | bytes 294920 | tf_op jit(solution)/shard_map/ppermute | solution.py:26
  34.4 4.5 collective-permute-start.7
  88.9 11.1 %collective-permute-start.8 = (f32[2,3,2,8,128]{4,3,2,1,0:T(8,128)S(1)}, f32[2,3,2,8,128]{4,3,2,1,0:T(8,128)S(1)}, u32[]{:S(2)}, u32[]{:S(2)}) collective-permute-start(f32[2,3,2,8,128]{4,3,2,1,0:T(8,128)S(1)} %get-tuple-element.295), channel_id=1, source_target_pairs={{16,0},{32,16},{48,32},{64,48},{80,64},{96,80},{112,96},{17,1},{33... | collective-permute-start | bytes 147464 | tf_op jit(solution)/shard_map/ppermute | solution.py:26
  90.2 9.8 %collective-permute-start.9 = (f32[2,3,2,8,128]{4,3,2,1,0:T(8,128)S(1)}, f32[2,3,2,8,128]{4,3,2,1,0:T(8,128)S(1)}, u32[]{:S(2)}, u32[]{:S(2)}) collective-permute-start(f32[2,3,2,8,128]{4,3,2,1,0:T(8,128)S(1)} %get-tuple-element.294), channel_id=1, source_target_pairs={{0,16},{16,32},{32,48},{48,64},{64,80},{80,96},{96,112},{1,17},{17... | collective-permute-start | bytes 147464 | tf_op jit(solution)/shard_map/ppermute | solution.py:25
  94.3 5.9 %collective-permute-start.10 = (f32[2,3,16,2,128]{4,3,2,1,0:T(2,128)S(1)}, f32[2,3,16,2,128]{4,3,2,1,0:T(2,128)S(1)}, u32[]{:S(2)}, u32[]{:S(2)}) collective-permute-start(f32[2,3,16,2,128]{4,3,2,1,0:T(2,128)S(1)} %get-tuple-element.297), channel_id=1, source_target_pairs={{1,0},{2,1},{3,2},{4,3},{5,4},{6,5},{7,6},{8,7},{9,8},{10,9},{11,1... | collective-permute-start | bytes 294920 | tf_op jit(solution)/shard_map/ppermute | solution.py:26
  147.9 11.0 %collective-permute-start.12 = (f32[2,3,2,8,128]{4,3,2,1,0:T(8,128)S(1)}, f32[2,3,2,8,128]{4,3,2,1,0:T(8,128)S(1)}, u32[]{:S(2)}, u32[]{:S(2)}) collective-permute-start(f32[2,3,2,8,128]{4,3,2,1,0:T(8,128)S(1)} %get-tuple-element.287), channel_id=1, source_target_pairs={{16,0},{32,16},{48,32},{64,48},{80,64},{96,80},{112,96},{17,1},{33... | collective-permute-start | bytes 147464 | tf_op jit(solution)/shard_map/ppermute | solution.py:26
  149.2 9.7 %collective-permute-start.13 = (f32[2,3,2,8,128]{4,3,2,1,0:T(8,128)S(1)}, f32[2,3,2,8,128]{4,3,2,1,0:T(8,128)S(1)}, u32[]{:S(2)}, u32[]{:S(2)}) collective-permute-start(f32[2,3,2,8,128]{4,3,2,1,0:T(8,128)S(1)} %get-tuple-element.286), channel_id=1, source_target_pairs={{0,16},{16,32},{32,48},{48,64},{64,80},{80,96},{96,112},{1,17},{17... | collective-permute-start | bytes 147464 | tf_op jit(solution)/shard_map/ppermute | solution.py:25
  153.3 5.9 %collective-permute-start.14 = (f32[2,3,16,2,128]{4,3,2,1,0:T(2,128)S(1)}, f32[2,3,16,2,128]{4,3,2,1,0:T(2,128)S(1)}, u32[]{:S(2)}, u32[]{:S(2)}) collective-permute-start(f32[2,3,16,2,128]{4,3,2,1,0:T(2,128)S(1)} %get-tuple-element.289), channel_id=1, source_target_pairs={{1,0},{2,1},{3,2},{4,3},{5,4},{6,5},{7,6},{8,7},{9,8},{10,9},{11,1... | collective-permute-start | bytes 294920 | tf_op jit(solution)/shard_map/ppermute | solution.py:26
  201.9 10.9 %collective-permute-start.16 = (f32[2,3,2,8,128]{4,3,2,1,0:T(8,128)S(1)}, f32[2,3,2,8,128]{4,3,2,1,0:T(8,128)S(1)}, u32[]{:S(2)}, u32[]{:S(2)}) collective-permute-start(f32[2,3,2,8,128]{4,3,2,1,0:T(8,128)S(1)} %get-tuple-element.281), channel_id=1, source_target_pairs={{16,0},{32,16},{48,32},{64,48},{80,64},{96,80},{112,96},{17,1},{33... | collective-permute-start | bytes 147464 | tf_op jit(solution)/shard_map/ppermute | solution.py:26
  203.2 9.7 %collective-permute-start.17 = (f32[2,3,2,8,128]{4,3,2,1,0:T(8,128)S(1)}, f32[2,3,2,8,128]{4,3,2,1,0:T(8,128)S(1)}, u32[]{:S(2)}, u32[]{:S(2)}) collective-permute-start(f32[2,3,2,8,128]{4,3,2,1,0:T(8,128)S(1)} %get-tuple-element.280), channel_id=1, source_target_pairs={{0,16},{16,32},{32,48},{48,64},{64,80},{80,96},{96,112},{1,17},{17... | collective-permute-start | bytes 147464 | tf_op jit(solution)/shard_map/ppermute | solution.py:25
  207.2 5.9 %collective-permute-start.18 = (f32[2,3,16,2,128]{4,3,2,1,0:T(2,128)S(1)}, f32[2,3,16,2,128]{4,3,2,1,0:T(2,128)S(1)}, u32[]{:S(2)}, u32[]{:S(2)}) collective-permute-start(f32[2,3,16,2,128]{4,3,2,1,0:T(2,128)S(1)} %get-tuple-element.283), channel_id=1, source_target_pairs={{1,0},{2,1},{3,2},{4,3},{5,4},{6,5},{7,6},{8,7},{9,8},{10,9},{11,1... | collective-permute-start | bytes 294920 | tf_op jit(solution)/shard_map/ppermute | solution.py:26
  210.1 4.4 collective-permute-start.19
  267.9 11.3 %collective-permute-start.20 = (f32[2,3,2,8,128]{4,3,2,1,0:T(8,128)S(1)}, f32[2,3,2,8,128]{4,3,2,1,0:T(8,128)S(1)}, u32[]{:S(2)}, u32[]{:S(2)}) collective-permute-start(f32[2,3,2,8,128]{4,3,2,1,0:T(8,128)S(1)} %get-tuple-element.273), channel_id=1, source_target_pairs={{16,0},{32,16},{48,32},{64,48},{80,64},{96,80},{112,96},{17,1},{33... | collective-permute-start | bytes 147464 | tf_op jit(solution)/shard_map/ppermute | solution.py:26
  269.2 10.1 %collective-permute-start.21 = (f32[2,3,2,8,128]{4,3,2,1,0:T(8,128)S(1)}, f32[2,3,2,8,128]{4,3,2,1,0:T(8,128)S(1)}, u32[]{:S(2)}, u32[]{:S(2)}) collective-permute-start(f32[2,3,2,8,128]{4,3,2,1,0:T(8,128)S(1)} %get-tuple-element.272), channel_id=1, source_target_pairs={{0,16},{16,32},{32,48},{48,64},{64,80},{80,96},{96,112},{1,17},{17... | collective-permute-start | bytes 147464 | tf_op jit(solution)/shard_map/ppermute | solution.py:25
  273.2 6.1 %collective-permute-start.22 = (f32[2,3,16,2,128]{4,3,2,1,0:T(2,128)S(1)}, f32[2,3,16,2,128]{4,3,2,1,0:T(2,128)S(1)}, u32[]{:S(2)}, u32[]{:S(2)}) collective-permute-start(f32[2,3,16,2,128]{4,3,2,1,0:T(2,128)S(1)} %get-tuple-element.275), channel_id=1, source_target_pairs={{1,0},{2,1},{3,2},{4,3},{5,4},{6,5},{7,6},{8,7},{9,8},{10,9},{11,1... | collective-permute-start | bytes 294920 | tf_op jit(solution)/shard_map/ppermute | solution.py:26
  276.1 4.4 collective-permute-start.23
  324.0 11.0 %collective-permute-start.24 = (f32[2,3,2,8,128]{4,3,2,1,0:T(8,128)S(1)}, f32[2,3,2,8,128]{4,3,2,1,0:T(8,128)S(1)}, u32[]{:S(2)}, u32[]{:S(2)}) collective-permute-start(f32[2,3,2,8,128]{4,3,2,1,0:T(8,128)S(1)} %get-tuple-element.267), channel_id=1, source_target_pairs={{16,0},{32,16},{48,32},{64,48},{80,64},{96,80},{112,96},{17,1},{33... | collective-permute-start | bytes 147464 | tf_op jit(solution)/shard_map/ppermute | solution.py:26
  325.3 9.7 %collective-permute-start.25 = (f32[2,3,2,8,128]{4,3,2,1,0:T(8,128)S(1)}, f32[2,3,2,8,128]{4,3,2,1,0:T(8,128)S(1)}, u32[]{:S(2)}, u32[]{:S(2)}) collective-permute-start(f32[2,3,2,8,128]{4,3,2,1,0:T(8,128)S(1)} %get-tuple-element.266), channel_id=1, source_target_pairs={{0,16},{16,32},{32,48},{48,64},{64,80},{80,96},{96,112},{1,17},{17... | collective-permute-start | bytes 147464 | tf_op jit(solution)/shard_map/ppermute | solution.py:25
  329.4 5.9 %collective-permute-start.26 = (f32[2,3,16,2,128]{4,3,2,1,0:T(2,128)S(1)}, f32[2,3,16,2,128]{4,3,2,1,0:T(2,128)S(1)}, u32[]{:S(2)}, u32[]{:S(2)}) collective-permute-start(f32[2,3,16,2,128]{4,3,2,1,0:T(2,128)S(1)} %get-tuple-element.269), channel_id=1, source_target_pairs={{1,0},{2,1},{3,2},{4,3},{5,4},{6,5},{7,6},{8,7},{9,8},{10,9},{11,1... | collective-permute-start | bytes 294920 | tf_op jit(solution)/shard_map/ppermute | solution.py:26
  332.2 4.4 collective-permute-start.27
  445.0 11.1 %collective-permute-start.28 = (f32[2,3,2,8,128]{4,3,2,1,0:T(8,128)S(1)}, f32[2,3,2,8,128]{4,3,2,1,0:T(8,128)S(1)}, u32[]{:S(2)}, u32[]{:S(2)}) collective-permute-start(f32[2,3,2,8,128]{4,3,2,1,0:T(8,128)S(1)} %get-tuple-element.259), channel_id=1, source_target_pairs={{16,0},{32,16},{48,32},{64,48},{80,64},{96,80},{112,96},{17,1},{33... | collective-permute-start | bytes 147464 | tf_op jit(solution)/shard_map/ppermute | solution.py:26
  446.3 9.8 %collective-permute-start.29 = (f32[2,3,2,8,128]{4,3,2,1,0:T(8,128)S(1)}, f32[2,3,2,8,128]{4,3,2,1,0:T(8,128)S(1)}, u32[]{:S(2)}, u32[]{:S(2)}) collective-permute-start(f32[2,3,2,8,128]{4,3,2,1,0:T(8,128)S(1)} %get-tuple-element.258), channel_id=1, source_target_pairs={{0,16},{16,32},{32,48},{48,64},{64,80},{80,96},{96,112},{1,17},{17... | collective-permute-start | bytes 147464 | tf_op jit(solution)/shard_map/ppermute | solution.py:25
  450.4 5.9 %collective-permute-start.30 = (f32[2,3,16,2,128]{4,3,2,1,0:T(2,128)S(1)}, f32[2,3,16,2,128]{4,3,2,1,0:T(2,128)S(1)}, u32[]{:S(2)}, u32[]{:S(2)}) collective-permute-start(f32[2,3,16,2,128]{4,3,2,1,0:T(2,128)S(1)} %get-tuple-element.261), channel_id=1, source_target_pairs={{1,0},{2,1},{3,2},{4,3},{5,4},{6,5},{7,6},{8,7},{9,8},{10,9},{11,1... | collective-permute-start | bytes 294920 | tf_op jit(solution)/shard_map/ppermute | solution.py:26
  502.0 11.0 %collective-permute-start.32 = (f32[2,3,2,8,128]{4,3,2,1,0:T(8,128)S(1)}, f32[2,3,2,8,128]{4,3,2,1,0:T(8,128)S(1)}, u32[]{:S(2)}, u32[]{:S(2)}) collective-permute-start(f32[2,3,2,8,128]{4,3,2,1,0:T(8,128)S(1)} %get-tuple-element.253), channel_id=1, source_target_pairs={{16,0},{32,16},{48,32},{64,48},{80,64},{96,80},{112,96},{17,1},{33... | collective-permute-start | bytes 147464 | tf_op jit(solution)/shard_map/ppermute | solution.py:26
  503.3 9.7 %collective-permute-start.33 = (f32[2,3,2,8,128]{4,3,2,1,0:T(8,128)S(1)}, f32[2,3,2,8,128]{4,3,2,1,0:T(8,128)S(1)}, u32[]{:S(2)}, u32[]{:S(2)}) collective-permute-start(f32[2,3,2,8,128]{4,3,2,1,0:T(8,128)S(1)} %get-tuple-element.252), channel_id=1, source_target_pairs={{0,16},{16,32},{32,48},{48,64},{64,80},{80,96},{96,112},{1,17},{17... | collective-permute-start | bytes 147464 | tf_op jit(solution)/shard_map/ppermute | solution.py:25
  507.4 5.9 %collective-permute-start.34 = (f32[2,3,16,2,128]{4,3,2,1,0:T(2,128)S(1)}, f32[2,3,16,2,128]{4,3,2,1,0:T(2,128)S(1)}, u32[]{:S(2)}, u32[]{:S(2)}) collective-permute-start(f32[2,3,16,2,128]{4,3,2,1,0:T(2,128)S(1)} %get-tuple-element.255), channel_id=1, source_target_pairs={{1,0},{2,1},{3,2},{4,3},{5,4},{6,5},{7,6},{8,7},{9,8},{10,9},{11,1... | collective-permute-start | bytes 294920 | tf_op jit(solution)/shard_map/ppermute | solution.py:26
  (49 other events, 449.9 us)
